TPU v7x, 256 devices: a whole 4x4x8 slice. The times are simulated.
256 devices in a mesh: row: 8 (over z), col: 16 (over y_lo, x, core), layer: 2 (over y_hi).
Axes of the slice: x: 4, y: 4 (y_hi: 2, y_lo: 2; y = y_hi * 2 + y_lo), z: 8, core: 2. Of those that a mesh axis runs over, the one named last changes fastest.
Arguments:
- left: bfloat16 [8192, 8192], P('row', ('col', 'layer')), may hold values from -6 to 6
- middle: bfloat16 [8192, 8192], P('row', 'col'), may hold values from -0.0625 to 0.0625
- right: bfloat16 [8192, 8192], P('row', 'col'), may hold values from -0.0625 to 0.0625
Outputs:
- product: bfloat16 [8192, 8192], P('row', ('col', 'layer'))
All inputs are finite; a program needn't handle non-finite values.
Results may differ from a plain program's by a relative error of at most 0.0049.
Values may be sent and summed in bfloat16 or wider, within the bound.
A program may use at most 64 MiB of HBM per device.

v0:
```python
import jax
import jax.numpy as jnp
from jax import lax
from jax.sharding import PartitionSpec as P


def split_up(array, dim, size):
    lengths = array.shape
    blocks = array.reshape(*lengths[:dim], size, lengths[dim] // size, *lengths[dim + 1 :])
    return jnp.moveaxis(blocks, dim, 0)


def sum_at_owner(array, axis, dim):
    blocks = split_up(array, dim, lax.axis_size(axis))
    arrived = lax.all_to_all(blocks, axis, split_axis=0, concat_axis=0, tiled=True)
    return arrived.sum(axis=0)


def multiply(left, right):
    width = left.shape[1]
    layers = lax.axis_size("layer")
    layer_index = lax.axis_index("layer")
    columns = right.shape[1]
    groups = right.shape[0] // width // layers
    shaped = right.reshape(groups, layers, width, columns)
    own_rows = lax.dynamic_index_in_dim(shaped, layer_index, 1, keepdims=False).reshape(
        groups * width, columns
    )
    right_all = lax.all_gather(own_rows, "row", axis=0, tiled=True)
    return jnp.dot(
        lax.all_gather(left, "col", axis=1, tiled=True),
        right_all,
        preferred_element_type=jnp.float32,
    )


def per_device(left, middle, right):
    partial_value = multiply(left, middle)
    first = sum_at_owner(partial_value, "layer", 1)
    first = first.astype(jnp.bfloat16)
    second = multiply(first, right)
    return sum_at_owner(second, "layer", 1).astype(jnp.bfloat16)


def solution(mesh):
    return jax.shard_map(
        per_device,
        mesh=mesh,
        in_specs=(P("row", ("col", "layer")), P("row", "col"), P("row", "col")),
        out_specs=P("row", ("col", "layer")),
        check_vma=False,
    )
```

profile of v0, /device:TPU:1, one launch (start us, length us, event | category | flops | bytes accessed | tf_op | source)
XLA Modules:
  0.0 290.7 jit_solution(16866077000397679622)
XLA Ops:
  6.5 0.0 copy-start
  6.5 0.0 all-gather.5.cloned.1.call-start
  6.5 1.2 copy-done
  7.8 0.8 constant_dynamic-slice_fusion.1
  8.6 0.0 all-gather.5.cloned.1.call-update
  8.6 0.0 all-gather.7.cloned.1.call-start
  8.7 0.7 all-gather.7.cloned.1.call-update
  9.4 0.0 all-gather.11.cloned.1.call-start
  9.4 1.9 constant_dynamic-slice_fusion
  11.3 0.0 all-gather.11.cloned.1.call-update
  11.3 0.0 all-gather.9.cloned.1.call-start
  11.4 56.2 %all-gather.5.cloned.1.call-done = bf16[4096,512]{1,0:T(8,128)(2,1)} async-done(((bf16[512,512]{1,0:T(8,128)(2,1)}), bf16[4096,512]{1,0:T(8,128)(2,1)}) %all-gather.5.cloned.1.call-update) | async-done | bytes 4194320 | tf_op jit(solution)/shard_map/all_gather | solution.py:29
  67.5 64.4 %all-gather.7.cloned.1.call-done = bf16[1024,4096]{1,0:T(8,128)(2,1)} async-done(((bf16[1024,256]{1,0:T(8,128)(2,1)}), bf16[1024,4096]{1,0:T(8,128)(2,1)}) %all-gather.7.cloned.1.call-update) | async-done | bytes 8388624 | tf_op jit(solution)/shard_map/all_gather | solution.py:31
  131.9 8.2 %fusion = f32[512,1024]{1,0:T(8,128)S(1)} fusion(bf16[4096,512]{1,0:T(8,128)(2,1)} %all-gather.5.cloned.1.call-done, bf16[1024,4096]{1,0:T(8,128)(2,1)} %all-gather.7.cloned.1.call-done), kind=kOutput, calls=%fused_computation.2 | convolution fusion | flops 4294967296 | bytes 14680064 | tf_op jit(solution)/shard_map/dot_general | solution.py:30
  140.1 28.8 %all_to_all.10 = f32[2,1024,256]{1,2,0:T(8,128)S(1)} all-to-all(f32[2,1024,256]{1,2,0:T(8,128)S(1)} %bitcast.17), channel_id=1, replica_groups=mesh['row'=8,'col'=16,'layer'=2] {'layer'}, dimensions={0} | all-to-all | bytes 4194304 | tf_op jit(solution)/shard_map/all_to_all | solution.py:15
  168.9 1.1 reduce_sum.18
  170.0 0.0 all-gather.9.cloned.1.call-update
  170.0 17.7 %all-gather.11.cloned.1.call-done = bf16[4096,512]{1,0:T(8,128)(2,1)} async-done(((bf16[512,512]{1,0:T(8,128)(2,1)}), bf16[4096,512]{1,0:T(8,128)(2,1)}) %all-gather.11.cloned.1.call-update) | async-done | bytes 4194320 | tf_op jit(solution)/shard_map/all_gather | solution.py:29
  187.7 55.5 %all-gather.9.cloned.1.call-done = bf16[1024,4096]{0,1:T(8,128)(2,1)} async-done(((bf16[1024,256]{0,1:T(8,128)(2,1)}), bf16[1024,4096]{0,1:T(8,128)(2,1)}) %all-gather.9.cloned.1.call-update) | async-done | bytes 8388624 | tf_op jit(solution)/shard_map/all_gather | solution.py:31
  243.2 8.2 %fusion.1 = f32[1024,512]{0,1:T(8,128)S(1)} fusion(bf16[1024,4096]{0,1:T(8,128)(2,1)} %all-gather.9.cloned.1.call-done, bf16[4096,512]{1,0:T(8,128)(2,1)} %all-gather.11.cloned.1.call-done), kind=kOutput, calls=%fused_computation.3 | convolution fusion | flops 4294967296 | bytes 14680064 | tf_op jit(solution)/shard_map/dot_general | solution.py:30
  251.4 29.6 %all_to_all.11 = f32[2,1024,256]{1,2,0:T(8,128)S(1)} all-to-all(f32[2,1024,256]{1,2,0:T(8,128)S(1)} %bitcast.18), channel_id=1, replica_groups=mesh['row'=8,'col'=16,'layer'=2] {'layer'}, dimensions={0} | all-to-all | bytes 4194304 | tf_op jit(solution)/shard_map/all_to_all | solution.py:15
  281.0 1.1 reduce_sum.19
  282.1 2.0 copy.4
Async XLA Ops:
  6.5 1.2 copy-start
  6.5 61.0 %all-gather.5.cloned.1.call-start = ((), (), s32[]{:S(2)}) async-start(), calls=%async_computation.2 | async-start | bytes 4718592 | tf_op jit(solution)/shard_map/all_gather | solution.py:29
  8.6 123.3 %all-gather.7.cloned.1.call-start = ((), (), s32[]{:S(2)}) async-start(), calls=%async_computation.3 | async-start | bytes 8912896 | tf_op jit(solution)/shard_map/all_gather | solution.py:31
  9.4 178.3 %all-gather.11.cloned.1.call-start = ((), (), s32[]{:S(2)}) async-start(), calls=%async_computation.5 | async-start | bytes 4718592 | tf_op jit(solution)/shard_map/all_gather | solution.py:29
  11.3 231.9 %all-gather.9.cloned.1.call-start = ((), (), s32[]{:S(2)}) async-start(), calls=%async_computation.4 | async-start | bytes 8912896 | tf_op jit(solution)/shard_map/all_gather | solution.py:31
Sparse Core Ops, SparseCore 0:
  9.1 58.3 all-gather.4
  69.3 62.5 all-gather.6
  133.7 53.9 all-gather.10
  189.4 53.7 all-gather.8
where the time goes:
time: 291 us
  waiting for transfers between devices  194 us (67%)
  blocking collectives  58.3 us (20%)
  matrix products  16.5 us (6%)
  between operations  13.1 us (5%)
  local copies, waits for them, and re-layouts  5.97 us (2%)
    all_gather x2, waiting for transfers between devices, multiply(): lax.all_gather(left, 'col', axis=1, tiled=True)  120 us
    all_gather x2, waiting for transfers between devices, multiply(): right_all = lax.all_gather(own_rows, 'row', axis=0, tiled=True)  73.8 us
    all_to_all x2, blocking collectives, sum_at_owner(): lax.all_to_all(blocks, axis, split_axis=0, concat_axis=0, tiled=True)  58.3 us
    dot_general x2, matrix products, multiply(): jnp.dot(lax.all_gather(left, 'col', axis=1, tiled=True), right_all, prefe...  16.5 us
  transfers between devices with their start and end apart: 4, of which 4 were waited for; matrix products, arithmetic and copies ran while one was open for 4% of the time, Pallas kernels for 0%

commit v1 on v0

--- a/solution.py
+++ b/solution.py
@@ -2,6 +2,28 @@
 import jax.numpy as jnp
 from jax import lax
 from jax.sharding import PartitionSpec as P
+
+
+def in_order(blocks, dim):
+    blocks = jnp.moveaxis(blocks, 0, dim)
+    dims = blocks.shape
+    return blocks.reshape(*dims[:dim], dims[dim] * dims[dim + 1], *dims[dim + 2 :])
+
+
+def gather_around(x, axis, dim):
+    size = lax.axis_size(axis)
+    pairs = [(i, (i + 1) % size) for i in range(size)]
+    back = [(b, a) for a, b in pairs]
+    lower, upper = ([], [])
+    for step in range(size - 1):
+        if step % 2 == 0:
+            lower.append(lax.ppermute(lower[-1] if lower else x, axis, pairs))
+        else:
+            upper.append(lax.ppermute(upper[-1] if upper else x, axis, back))
+    blocks = jnp.stack([*lower[::-1], x, *upper])
+    shift = lax.axis_index(axis) - len(lower)
+    blocks = blocks[(jnp.arange(size) - shift) % size]
+    return in_order(blocks, dim)
 
 
 def split_up(array, dim, size):
@@ -26,7 +48,7 @@
     own_rows = lax.dynamic_index_in_dim(shaped, layer_index, 1, keepdims=False).reshape(
         groups * width, columns
     )
-    right_all = lax.all_gather(own_rows, "row", axis=0, tiled=True)
+    right_all = gather_around(own_rows, "row", 0)
     return jnp.dot(
         lax.all_gather(left, "col", axis=1, tiled=True),
         right_all,

time: 291 us -> 226 us (0.78)
  the two profiles are of different devices: /device:TPU:1 before, /device:TPU:2 now
where the time goes in v1:
time: 226 us
  waiting for transfers between devices  87 us (38%)
  blocking collectives  47.7 us (21%)
  local copies, waits for them, and re-layouts  36.6 us (16%)
  starting transfers between devices  22.3 us (10%)
  matrix products  16.4 us (7%)
  between operations  13.5 us (6%)
    ppermute x8, waiting for transfers between devices, gather_around(): lower.append(lax.ppermute(lower[-1] if lower else x, axis, pairs))  86.2 us
    all_to_all x2, blocking collectives, sum_at_owner(): lax.all_to_all(blocks, axis, split_axis=0, concat_axis=0, tiled=True)  47.7 us
    ppermute x6, starting transfers between devices, gather_around(): upper.append(lax.ppermute(upper[-1] if upper else x, axis, back))  20.2 us
    dot_general x2, matrix products, multiply(): jnp.dot(lax.all_gather(left, 'col', axis=1, tiled=True), right_all, prefe...  16.4 us
    unnamed x16, local copies, waits for them, and re-layouts  15.4 us
    gather x2, local copies, waits for them, and re-layouts, gather_around(): blocks = blocks[(jnp.arange(size) - shift) % size]  10 us
    dot_general x1, local copies, waits for them, and re-layouts, multiply(): jnp.dot(lax.all_gather(left, 'col', axis=1, tiled=True), right_all, prefe...  6.34 us
  transfers between devices with their start and end apart: 16, of which 9 were waited for; matrix products, arithmetic and copies ran while one was open for 15% of the time, Pallas kernels for 0%

profile of v1, /device:TPU:2, one launch (start us, length us, event | category | flops | bytes accessed | tf_op | source)
XLA Modules:
  0.0 225.7 jit_solution(6099649152393571983)
XLA Ops:
  6.5 0.7 all-gather.3.cloned.1.call-update
  7.3 0.0 all-gather.5.cloned.1.call-start
  7.3 0.5 copy-done
  7.8 2.0 collective-permute-start
  9.8 15.9 %collective-permute-done = bf16[512,512]{1,0:T(8,128)(2,1)S(1)} collective-permute-done((bf16[512,512]{1,0:T(8,128)(2,1)S(1)}, bf16[512,512]{1,0:T(8,128)(2,1)S(1)}, u32[]{:S(2)}, u32[]{:S(2)}) %collective-permute-start) | collective-permute-done | bytes 524320 | tf_op jit(solution)/shard_map/ppermute | solution.py:20
  25.7 3.2 %collective-permute-start.4 = (bf16[512,512]{1,0:T(8,128)(2,1)S(1)}, bf16[512,512]{1,0:T(8,128)(2,1)S(1)}, u32[]{:S(2)}, u32[]{:S(2)}) collective-permute-start(bf16[512,512]{1,0:T(8,128)(2,1)S(1)} %bitcast.65), channel_id=1, source_target_pairs={{32,0},{64,32},{96,64},{128,96},{160,128},{192,160},{224,192},{0,2... | collective-permute-start | bytes 1572872 | tf_op jit(solution)/shard_map/ppermute | solution.py:22
  28.9 11.1 %collective-permute-done.1 = bf16[512,512]{1,0:T(8,128)(2,1)S(1)} collective-permute-done((bf16[512,512]{1,0:T(8,128)(2,1)S(1)}, bf16[512,512]{1,0:T(8,128)(2,1)S(1)}, u32[]{:S(2)}, u32[]{:S(2)}) %collective-permute-start.1) | collective-permute-done | bytes 524320 | tf_op jit(solution)/shard_map/ppermute | solution.py:20
  40.0 3.2 %collective-permute-start.5 = (bf16[512,512]{1,0:T(8,128)(2,1)S(1)}, bf16[512,512]{1,0:T(8,128)(2,1)}, u32[]{:S(2)}, u32[]{:S(2)}) collective-permute-start(bf16[512,512]{1,0:T(8,128)(2,1)S(1)} %collective-permute-done.4), channel_id=1, source_target_pairs={{32,0},{64,32},{96,64},{128,96},{160,128},{192,160},{224,192},{0,2... | collective-permute-start | bytes 1572872 | tf_op jit(solution)/shard_map/ppermute | solution.py:22
  43.2 10.3 %collective-permute-done.2 = bf16[512,512]{1,0:T(8,128)(2,1)} collective-permute-done((bf16[512,512]{1,0:T(8,128)(2,1)S(1)}, bf16[512,512]{1,0:T(8,128)(2,1)}, u32[]{:S(2)}, u32[]{:S(2)}) %collective-permute-start.2) | collective-permute-done | bytes 524320 | tf_op jit(solution)/shard_map/ppermute | solution.py:20
  53.5 3.3 %collective-permute-start.6 = (bf16[512,512]{1,0:T(8,128)(2,1)}, bf16[512,512]{1,0:T(8,128)(2,1)S(1)}, u32[]{:S(2)}, u32[]{:S(2)}) collective-permute-start(bf16[512,512]{1,0:T(8,128)(2,1)} %collective-permute-done.5), channel_id=1, source_target_pairs={{32,0},{64,32},{96,64},{128,96},{160,128},{192,160},{224,192},{0,2... | collective-permute-start | bytes 1572872 | tf_op jit(solution)/shard_map/ppermute | solution.py:22
  56.9 9.6 %collective-permute-done.3 = bf16[512,512]{1,0:T(8,128)(2,1)} collective-permute-done((bf16[512,512]{1,0:T(8,128)(2,1)}, bf16[512,512]{1,0:T(8,128)(2,1)}, u32[]{:S(2)}, u32[]{:S(2)}) %collective-permute-start.3) | collective-permute-done | bytes 524320 | tf_op jit(solution)/shard_map/ppermute | solution.py:20
  66.4 1.9 bitcast_dynamic-update-slice_fusion.13
  68.3 1.9 bitcast_dynamic-update-slice_fusion.12
  70.2 0.8 bitcast_dynamic-update-slice_fusion.11
  71.1 0.8 bitcast_dynamic-update-slice_fusion.10
  71.9 0.8 constant_dynamic-update-slice_fusion
  72.7 0.8 bitcast_dynamic-update-slice_fusion.9
  73.6 1.9 bitcast_dynamic-update-slice_fusion.8
  75.5 0.8 bitcast_dynamic-update-slice_fusion.7
  76.3 4.9 %gather_fusion = bf16[8,512,512]{2,1,0:T(8,128)(2,1)} fusion(bf16[8,512,512]{2,1,0:T(8,128)(2,1)} %bitcast_dynamic-update-slice_fusion.7, s32[1024]{0:T(1024)S(1)} %pad_clamp_fusion), kind=kCustom, calls=%fused_computation | custom fusion | bytes 8388640 | tf_op jit(solution)/shard_map/gather | solution.py:25
  81.2 8.2 %fusion.7 = f32[512,1024]{1,0:T(8,128)S(1)} fusion(bf16[4096,512]{1,0:T(8,128)(2,1)} %bitcast.62, bf16[1024,4096]{1,0:T(8,128)(2,1)} %all-gather.3.cloned.1.call-done), kind=kOutput, calls=%fused_computation.30 | convolution fusion | flops 4294967296 | bytes 14680064 | tf_op jit(solution)/shard_map/dot_general | solution.py:52
  89.5 27.4 %all_to_all.10 = f32[2,1024,256]{1,2,0:T(8,128)S(1)} all-to-all(f32[2,1024,256]{1,2,0:T(8,128)S(1)} %bitcast.63), channel_id=1, replica_groups=mesh['row'=8,'col'=16,'layer'=2] {'layer'}, dimensions={0} | all-to-all | bytes 4194304 | tf_op jit(solution)/shard_map/all_to_all | solution.py:37
  116.9 1.1 reduce_sum.18
  118.0 2.0 copy.6
  120.0 0.0 all-gather.5.cloned.1.call-update
  120.0 1.1 constant_dynamic-slice_fusion
  121.1 0.1 collective-permute-start.7
  121.2 12.1 %collective-permute-done.7 = bf16[512,512]{1,0:T(8,128)(2,1)S(1)} collective-permute-done((bf16[512,512]{1,0:T(8,128)(2,1)S(1)}, bf16[512,512]{1,0:T(8,128)(2,1)S(1)}, u32[]{:S(2)}, u32[]{:S(2)}) %collective-permute-start.7) | collective-permute-done | bytes 524320 | tf_op jit(solution)/shard_map/ppermute | solution.py:20
  133.3 3.2 %collective-permute-start.11 = (bf16[512,512]{1,0:T(8,128)(2,1)S(1)}, bf16[512,512]{1,0:T(8,128)(2,1)S(1)}, u32[]{:S(2)}, u32[]{:S(2)}) collective-permute-start(bf16[512,512]{1,0:T(8,128)(2,1)S(1)} %bitcast.68), channel_id=1, source_target_pairs={{32,0},{64,32},{96,64},{128,96},{160,128},{192,160},{224,192},{0,2... | collective-permute-start | bytes 1572872 | tf_op jit(solution)/shard_map/ppermute | solution.py:22
  136.5 9.9 %collective-permute-done.8 = bf16[512,512]{1,0:T(8,128)(2,1)S(1)} collective-permute-done((bf16[512,512]{1,0:T(8,128)(2,1)S(1)}, bf16[512,512]{1,0:T(8,128)(2,1)S(1)}, u32[]{:S(2)}, u32[]{:S(2)}) %collective-permute-start.8) | collective-permute-done | bytes 524320 | tf_op jit(solution)/shard_map/ppermute | solution.py:20
  146.4 3.5 %collective-permute-start.12 = (bf16[512,512]{1,0:T(8,128)(2,1)S(1)}, bf16[512,512]{1,0:T(8,128)(2,1)S(1)}, u32[]{:S(2)}, u32[]{:S(2)}) collective-permute-start(bf16[512,512]{1,0:T(8,128)(2,1)S(1)} %collective-permute-done.11), channel_id=1, source_target_pairs={{32,0},{64,32},{96,64},{128,96},{160,128},{192,160},{224,192},{0,2... | collective-permute-start | bytes 1572872 | tf_op jit(solution)/shard_map/ppermute | solution.py:22
  150.0 10.8 %collective-permute-done.9 = bf16[512,512]{1,0:T(8,128)(2,1)S(1)} collective-permute-done((bf16[512,512]{1,0:T(8,128)(2,1)S(1)}, bf16[512,512]{1,0:T(8,128)(2,1)S(1)}, u32[]{:S(2)}, u32[]{:S(2)}) %collective-permute-start.9) | collective-permute-done | bytes 524320 | tf_op jit(solution)/shard_map/ppermute | solution.py:20
  160.7 0.1 collective-permute-done.12
  160.8 3.7 %collective-permute-start.13 = (bf16[512,512]{1,0:T(8,128)(2,1)S(1)}, bf16[512,512]{1,0:T(8,128)(2,1)S(1)}, u32[]{:S(2)}, u32[]{:S(2)}) collective-permute-start(bf16[512,512]{1,0:T(8,128)(2,1)S(1)} %collective-permute-done.12), channel_id=1, source_target_pairs={{32,0},{64,32},{96,64},{128,96},{160,128},{192,160},{224,192},{0,2... | collective-permute-start | bytes 1572872 | tf_op jit(solution)/shard_map/ppermute | solution.py:22
  164.5 6.6 %collective-permute-done.10 = bf16[512,512]{1,0:T(8,128)(2,1)S(1)} collective-permute-done((bf16[512,512]{1,0:T(8,128)(2,1)S(1)}, bf16[512,512]{1,0:T(8,128)(2,1)S(1)}, u32[]{:S(2)}, u32[]{:S(2)}) %collective-permute-start.10) | collective-permute-done | bytes 524320 | tf_op jit(solution)/shard_map/ppermute | solution.py:20
  171.1 0.9 bitcast_dynamic-update-slice_fusion.6
  172.0 0.8 bitcast_dynamic-update-slice_fusion.5
  172.8 0.8 bitcast_dynamic-update-slice_fusion.4
  173.7 0.8 bitcast_dynamic-update-slice_fusion.3
  174.5 0.8 constant_dynamic-update-slice_fusion.1
  175.4 0.8 bitcast_dynamic-update-slice_fusion.2
  176.2 0.8 bitcast_dynamic-update-slice_fusion.1
  177.0 0.8 bitcast_dynamic-update-slice_fusion
  177.9 5.1 %gather_fusion.1 = bf16[8,512,512]{2,1,0:T(8,128)(2,1)} fusion(bf16[8,512,512]{2,1,0:T(8,128)(2,1)} %bitcast_dynamic-update-slice_fusion, s32[1024]{0:T(1024)S(1)} %pad_clamp_fusion), kind=kCustom, calls=%fused_computation.1 | custom fusion | bytes 8388640 | tf_op jit(solution)/shard_map/gather | solution.py:25
  183.0 6.3 %copy.8 = bf16[512,4096]{1,0:T(8,128)(2,1)} copy(bf16[512,4096]{0,1:T(8,128)(2,1)} %bitcast.60) | data formatting | bytes 8388608 | tf_op jit(solution)/shard_map/dot_general | solution.py:52
  189.3 8.2 %fusion.2 = f32[2,1024,256]{2,1,0:T(8,128)S(1)} fusion(bf16[2,256,4096]{2,1,0:T(8,128)(2,1)} %bitcast.61, bf16[1024,4096]{1,0:T(8,128)(2,1)} %all-gather.5.cloned.1.call-done), kind=kOutput, calls=%fused_computation.4 | convolution fusion | flops 4294967296 | bytes 14680064 | tf_op jit(solution)/shard_map/dot_general | solution.py:52
  197.5 20.3 %all_to_all.11 = f32[2,1024,256]{2,1,0:T(8,128)S(1)} all-to-all(f32[2,1024,256]{2,1,0:T(8,128)S(1)} %fusion.2), channel_id=1, replica_groups=mesh['row'=8,'col'=16,'layer'=2] {'layer'}, dimensions={0} | all-to-all | bytes 4194304 | tf_op jit(solution)/shard_map/all_to_all | solution.py:37
  217.8 1.1 reduce_sum.19
  (18 shorter events, 0.1 us)
Async XLA Ops:
  6.5 1.2 copy-start
  6.5 74.7 %all-gather.3.cloned.1.call-start = ((), (), s32[]{:S(2)}) async-start(), calls=%async_computation.2 | async-start | bytes 8912896 | tf_op jit(solution)/shard_map/all_gather | solution.py:53
  7.3 182.0 %all-gather.5.cloned.1.call-start = ((), (), s32[]{:S(2)}) async-start(), calls=%async_computation.3 | async-start | bytes 8912896 | tf_op jit(solution)/shard_map/all_gather | solution.py:53
  7.8 17.9 %collective-permute-start = (bf16[512,512]{1,0:T(8,128)(2,1)S(1)}, bf16[512,512]{1,0:T(8,128)(2,1)S(1)}, u32[]{:S(2)}, u32[]{:S(2)}) collective-permute-start(bf16[512,512]{1,0:T(8,128)(2,1)S(1)} %bitcast.64), channel_id=1, source_target_pairs={{0,32},{32,64},{64,96},{96,128},{128,160},{160,192},{192,224},{224... | collective-permute-start | bytes 1572872 | tf_op jit(solution)/shard_map/ppermute | solution.py:20
  25.7 14.3 %collective-permute-start.1 = (bf16[512,512]{1,0:T(8,128)(2,1)S(1)}, bf16[512,512]{1,0:T(8,128)(2,1)S(1)}, u32[]{:S(2)}, u32[]{:S(2)}) collective-permute-start(bf16[512,512]{1,0:T(8,128)(2,1)S(1)} %collective-permute-done), channel_id=1, source_target_pairs={{0,32},{32,64},{64,96},{96,128},{128,160},{160,192},{192,224},{224... | collective-permute-start | bytes 1572872 | tf_op jit(solution)/shard_map/ppermute | solution.py:20
  25.7 14.3 %collective-permute-start.4 = (bf16[512,512]{1,0:T(8,128)(2,1)S(1)}, bf16[512,512]{1,0:T(8,128)(2,1)S(1)}, u32[]{:S(2)}, u32[]{:S(2)}) collective-permute-start(bf16[512,512]{1,0:T(8,128)(2,1)S(1)} %bitcast.65), channel_id=1, source_target_pairs={{32,0},{64,32},{96,64},{128,96},{160,128},{192,160},{224,192},{0,2... | collective-permute-start | bytes 1572872 | tf_op jit(solution)/shard_map/ppermute | solution.py:22
  40.0 13.5 %collective-permute-start.2 = (bf16[512,512]{1,0:T(8,128)(2,1)S(1)}, bf16[512,512]{1,0:T(8,128)(2,1)}, u32[]{:S(2)}, u32[]{:S(2)}) collective-permute-start(bf16[512,512]{1,0:T(8,128)(2,1)S(1)} %collective-permute-done.1), channel_id=1, source_target_pairs={{0,32},{32,64},{64,96},{96,128},{128,160},{160,192},{192,224},{224... | collective-permute-start | bytes 1572872 | tf_op jit(solution)/shard_map/ppermute | solution.py:20
  40.0 13.6 %collective-permute-start.5 = (bf16[512,512]{1,0:T(8,128)(2,1)S(1)}, bf16[512,512]{1,0:T(8,128)(2,1)}, u32[]{:S(2)}, u32[]{:S(2)}) collective-permute-start(bf16[512,512]{1,0:T(8,128)(2,1)S(1)} %collective-permute-done.4), channel_id=1, source_target_pairs={{32,0},{64,32},{96,64},{128,96},{160,128},{192,160},{224,192},{0,2... | collective-permute-start | bytes 1572872 | tf_op jit(solution)/shard_map/ppermute | solution.py:22
  53.5 12.9 %collective-permute-start.3 = (bf16[512,512]{1,0:T(8,128)(2,1)}, bf16[512,512]{1,0:T(8,128)(2,1)}, u32[]{:S(2)}, u32[]{:S(2)}) collective-permute-start(bf16[512,512]{1,0:T(8,128)(2,1)} %collective-permute-done.2), channel_id=1, source_target_pairs={{0,32},{32,64},{64,96},{96,128},{128,160},{160,192},{192,224},{224... | collective-permute-start | bytes 1572872 | tf_op jit(solution)/shard_map/ppermute | solution.py:20
  53.5 21.9 %collective-permute-start.6 = (bf16[512,512]{1,0:T(8,128)(2,1)}, bf16[512,512]{1,0:T(8,128)(2,1)S(1)}, u32[]{:S(2)}, u32[]{:S(2)}) collective-permute-start(bf16[512,512]{1,0:T(8,128)(2,1)} %collective-permute-done.5), channel_id=1, source_target_pairs={{32,0},{64,32},{96,64},{128,96},{160,128},{192,160},{224,192},{0,2... | collective-permute-start | bytes 1572872 | tf_op jit(solution)/shard_map/ppermute | solution.py:22
  121.1 12.2 %collective-permute-start.7 = (bf16[512,512]{1,0:T(8,128)(2,1)S(1)}, bf16[512,512]{1,0:T(8,128)(2,1)S(1)}, u32[]{:S(2)}, u32[]{:S(2)}) collective-permute-start(bf16[512,512]{1,0:T(8,128)(2,1)S(1)} %bitcast.67), channel_id=1, source_target_pairs={{0,32},{32,64},{64,96},{96,128},{128,160},{160,192},{192,224},{224... | collective-permute-start | bytes 1572872 | tf_op jit(solution)/shard_map/ppermute | solution.py:20
  133.3 13.1 %collective-permute-start.8 = (bf16[512,512]{1,0:T(8,128)(2,1)S(1)}, bf16[512,512]{1,0:T(8,128)(2,1)S(1)}, u32[]{:S(2)}, u32[]{:S(2)}) collective-permute-start(bf16[512,512]{1,0:T(8,128)(2,1)S(1)} %collective-permute-done.7), channel_id=1, source_target_pairs={{0,32},{32,64},{64,96},{96,128},{128,160},{160,192},{192,224},{224... | collective-permute-start | bytes 1572872 | tf_op jit(solution)/shard_map/ppermute | solution.py:20
  133.3 13.1 %collective-permute-start.11 = (bf16[512,512]{1,0:T(8,128)(2,1)S(1)}, bf16[512,512]{1,0:T(8,128)(2,1)S(1)}, u32[]{:S(2)}, u32[]{:S(2)}) collective-permute-start(bf16[512,512]{1,0:T(8,128)(2,1)S(1)} %bitcast.68), channel_id=1, source_target_pairs={{32,0},{64,32},{96,64},{128,96},{160,128},{192,160},{224,192},{0,2... | collective-permute-start | bytes 1572872 | tf_op jit(solution)/shard_map/ppermute | solution.py:22
  146.4 14.3 %collective-permute-start.9 = (bf16[512,512]{1,0:T(8,128)(2,1)S(1)}, bf16[512,512]{1,0:T(8,128)(2,1)S(1)}, u32[]{:S(2)}, u32[]{:S(2)}) collective-permute-start(bf16[512,512]{1,0:T(8,128)(2,1)S(1)} %collective-permute-done.8), channel_id=1, source_target_pairs={{0,32},{32,64},{64,96},{96,128},{128,160},{160,192},{192,224},{224... | collective-permute-start | bytes 1572872 | tf_op jit(solution)/shard_map/ppermute | solution.py:20
  146.4 14.4 %collective-permute-start.12 = (bf16[512,512]{1,0:T(8,128)(2,1)S(1)}, bf16[512,512]{1,0:T(8,128)(2,1)S(1)}, u32[]{:S(2)}, u32[]{:S(2)}) collective-permute-start(bf16[512,512]{1,0:T(8,128)(2,1)S(1)} %collective-permute-done.11), channel_id=1, source_target_pairs={{32,0},{64,32},{96,64},{128,96},{160,128},{192,160},{224,192},{0,2... | collective-permute-start | bytes 1572872 | tf_op jit(solution)/shard_map/ppermute | solution.py:22
  160.7 10.4 %collective-permute-start.10 = (bf16[512,512]{1,0:T(8,128)(2,1)S(1)}, bf16[512,512]{1,0:T(8,128)(2,1)S(1)}, u32[]{:S(2)}, u32[]{:S(2)}) collective-permute-start(bf16[512,512]{1,0:T(8,128)(2,1)S(1)} %collective-permute-done.9), channel_id=1, source_target_pairs={{0,32},{32,64},{64,96},{96,128},{128,160},{160,192},{192,224},{224... | collective-permute-start | bytes 1572872 | tf_op jit(solution)/shard_map/ppermute | solution.py:20
  160.8 16.2 %collective-permute-start.13 = (bf16[512,512]{1,0:T(8,128)(2,1)S(1)}, bf16[512,512]{1,0:T(8,128)(2,1)S(1)}, u32[]{:S(2)}, u32[]{:S(2)}) collective-permute-start(bf16[512,512]{1,0:T(8,128)(2,1)S(1)} %collective-permute-done.12), channel_id=1, source_target_pairs={{32,0},{64,32},{96,64},{128,96},{160,128},{192,160},{224,192},{0,2... | collective-permute-start | bytes 1572872 | tf_op jit(solution)/shard_map/ppermute | solution.py:22
Sparse Core Ops, SparseCore 0:
  9.1 65.8 all-gather.2
  120.2 59.6 all-gather.4
